TPU v7x, 512 devices: a whole 4x8x8 slice. The times are simulated.
512 devices in a mesh: dp: 64 (over y, x, z_lo), feat: 8 (over z_hi, core).
Axes of the slice: x: 4, y: 8, z: 8 (z_hi: 4, z_lo: 2; z = z_hi * 2 + z_lo), core: 2. Of those that a mesh axis runs over, the one named last changes fastest.
Arguments:
- embeddings: bfloat16 [327680, 2048], P('dp', 'feat'), may hold values from -80 to 80
- slot_image: int32 [327680], P('dp'), may hold values from 0 to 32767, as said below
- slot_view: int32 [327680], P('dp'), may hold values from 0 to 10, as said below
- pair_table: int32 [2, 2], replicated, may hold values from 0 to 9, as said below
Outputs:
- correlation: float32 [2, 2048, 2048], P(None, 'feat', 'dp')
Inputs may be any that keep to these rules, and one draw needn't show every extreme that they name: `slot_image`: image ids of dp index d run from d * 512 to (d + 1) * 512 - 1. Each image has views 0 and 1 and local views 2 to 1 + k with k from 1 to 8; the first image of every dp index has all 10 views; every (image, view) stands in one slot at most; empty slots name an image of their own dp index. `slot_view`: empty slots carry view 10 and come after the used slots of their dp index; the last dp index fills all its slots. `pair_table`: each pair's first view is global (0 or 1) and its second view differs from it.
All inputs are finite; a program needn't handle non-finite values.
Results may differ from a plain program's by a relative error of at most 0.00035.
Values may be sent and summed in bfloat16 or wider, within the bound.
A program may use at most 64 MiB of HBM per device.

v0:
```python
import jax
import jax.numpy as jnp
from jax import lax
from jax.sharding import Mesh
from jax.sharding import PartitionSpec as P

WIN = 2048
IMG_DEV = 512
PAIRS = 2
FEAT = ("feat_0", "feat_1")
DP = ("dp_0", "dp_1", "dp_2")
DP_FEAT = ("dp_0", "dp_1", "dp_2", "feat_0", "feat_1")
EPS = 1e-05


def one_axis_at_a_time(array, axes):
    for axis in axes:
        array = lax.psum(array, axis)
    return array


def split_up(array, dim, peers):
    before, after = (array.shape[:dim], array.shape[dim + 1 :])
    return jnp.moveaxis(array.reshape(*before, peers, -1, *after), dim, 0)


def summed_on_arrival(array, axis, dim):
    parts = split_up(array, dim, lax.axis_size(axis))
    arrived = lax.all_to_all(parts, axis, split_axis=0, concat_axis=0, tiled=True)
    return arrived.sum(axis=0)


def select_rows(embeddings, local_image, slot_view, view_id):
    image_grid = jnp.arange(IMG_DEV, dtype=jnp.int32)[:, None]
    selection = ((local_image[None, :] == image_grid) & (slot_view[None, :] == view_id)).astype(
        jnp.bfloat16
    )
    found = jnp.sum(selection.astype(jnp.float32), axis=1) > 0.5
    rows = jnp.dot(selection, embeddings, preferred_element_type=jnp.float32).astype(jnp.bfloat16)
    return (rows, found)


def image_product(columns, first_rows):
    return lax.dot_general(
        columns, first_rows, (((0,), (0,)), ((), ())), preferred_element_type=jnp.float32
    )


def local(embeddings, slot_image, slot_view, pair_table):
    width_local = embeddings.shape[1]
    feat_offset = lax.axis_index(FEAT) * width_local
    out_rows = WIN // lax.axis_size(DP)
    dp_offset = lax.axis_index(DP) * out_rows
    local_image = slot_image - lax.axis_index(DP) * IMG_DEV
    zeros_wide = jnp.zeros((WIN,), jnp.float32)
    outputs = []
    for pair_index in range(PAIRS):
        first_taken, first_found = select_rows(
            embeddings, local_image, slot_view, pair_table[pair_index, 0]
        )
        second_taken, second_found = select_rows(
            embeddings, local_image, slot_view, pair_table[pair_index, 1]
        )
        present = first_found & second_found
        first_rows = jnp.where(present[:, None], first_taken, jnp.zeros((), jnp.bfloat16))
        second_rows = jnp.where(present[:, None], second_taken, jnp.zeros((), jnp.bfloat16))
        first_wide = first_rows.astype(jnp.float32)
        second_wide = second_rows.astype(jnp.float32)
        images_here = jnp.sum(present.astype(jnp.float32))
        images_term = jnp.where(lax.axis_index(FEAT) == 0, images_here, jnp.zeros((), jnp.float32))

        def widen(vector):
            return lax.dynamic_update_slice_in_dim(zeros_wide, vector, feat_offset, 0)

        sum_first, sumsq_first, sum_second, sumsq_second, total = (
            one_axis_at_a_time(widen(jnp.sum(first_wide, axis=0)), DP_FEAT),
            one_axis_at_a_time(widen(jnp.sum(first_wide * first_wide, axis=0)), DP_FEAT),
            one_axis_at_a_time(widen(jnp.sum(second_wide, axis=0)), DP_FEAT),
            one_axis_at_a_time(widen(jnp.sum(second_wide * second_wide, axis=0)), DP_FEAT),
            one_axis_at_a_time(images_term, DP_FEAT),
        )
        partial_value = image_product(
            lax.all_gather(second_rows, FEAT, axis=1, tiled=True), first_rows
        )
        reduced = summed_on_arrival(partial_value, DP, 0)
        mean_first = lax.dynamic_slice_in_dim(sum_first, feat_offset, width_local, 0) / total
        square_first = lax.dynamic_slice_in_dim(sumsq_first, feat_offset, width_local, 0) / total
        mean_second = lax.dynamic_slice_in_dim(sum_second, dp_offset, out_rows, 0) / total
        square_second = lax.dynamic_slice_in_dim(sumsq_second, dp_offset, out_rows, 0) / total
        spread_first = jnp.sqrt(square_first - mean_first * mean_first + EPS)
        spread_second = jnp.sqrt(square_second - mean_second * mean_second + EPS)
        cross = reduced.T
        block = (cross / total - mean_first[:, None] * mean_second[None, :]) / (
            spread_first[:, None] * spread_second[None, :]
        )
        outputs.append(block)
    return jnp.stack(outputs, axis=0)


def solution(mesh):
    split = Mesh(mesh.devices.reshape(8, 4, 2, 4, 2), ("dp_0", "dp_1", "dp_2", "feat_0", "feat_1"))
    placed = (P(DP, FEAT), P(DP), P(DP), P())
    return jax.shard_map(
        local, mesh=split, in_specs=placed, out_specs=P(None, FEAT, DP), check_vma=False
    )
```

profile of v0, /device:TPU:1, one launch (start us, length us, event | category | flops | bytes accessed | tf_op | source)
XLA Modules:
  0.0 296.6 jit_solution(17913414915544847246)
XLA Ops:
  6.5 1.5 fusion.56
  8.0 0.7 broadcast_subtract_fusion
  8.7 3.3 %broadcast_compare_fusion.2 = (pred[5120]{0:T(1024)(128)(4,1)S(1)}, pred[5120]{0:T(1024)(128)(4,1)S(1)}, pred[5120]{0:T(1024)(128)(4,1)S(1)}, pred[5120]{0:T(1024)(128)(4,1)S(1)}) fusion(s32[5120]{0:T(1024)} %param.6, s32[]{:T(128)} %bitcast.1, s32[]{:T(128)} %bitcast, s32[]{:T(128)} %bitcast.6, s32[]{:T(128)} %bitcast.5), kind=kLoop, calls=%fused_computation.54 | loop fusion | flops 20480 | bytes 40976 | tf_op jit(solution)/shard_map/eq | solution.py:35
  12.0 5.7 %convert_reduce_fusion.3 = (f32[512]{0:T(512)S(1)}, f32[512]{0:T(512)S(1)}, f32[512]{0:T(512)S(1)}, f32[512]{0:T(512)S(1)}) fusion(s32[5120]{0:T(1024)S(1)} %broadcast_subtract_fusion, pred[5120]{0:T(1024)(128)(4,1)S(1)} %get-tuple-element.80, pred[5120]{0:T(1024)(128)(4,1)S(1)} %get-tuple-element.81, pred[5120]{0:T(1024)(128)(4,1)S(1)} %get-tuple-element.82, ...), kind=kLoop, calls=%fused_computation.3 | loop fusion | flops 44562432 | bytes 49152 | tf_op jit(solution)/shard_map/reduce_sum | solution.py:38
  17.7 0.6 convert_reduce_fusion.8
  18.3 2.8 fusion.51
  21.1 2.0 fusion.50
  23.1 47.3 %all-gather.5.cloned.1.call-done = bf16[512,2048]{1,0:T(8,128)(2,1)} async-done(((bf16[512,256]{1,0:T(8,128)(2,1)}), bf16[512,2048]{1,0:T(8,128)(2,1)}) %all-gather.5.cloned.1.call-update) | async-done | bytes 2097168 | tf_op jit(solution)/shard_map/all_gather | solution.py:83
  70.4 3.7 %fusion.58 = f32[2048,256]{1,0:T(8,128)} fusion(bf16[512,2048]{1,0:T(8,128)(2,1)} %all-gather.5.cloned.1.call-done, bf16[512,256]{1,0:T(8,128)(2,1)S(1)} %get-tuple-element.88), kind=kOutput, calls=%fused_computation.75 | convolution fusion | flops 536870912 | bytes 4456448 | tf_op jit(solution)/shard_map/dot_general | solution.py:44
  74.0 11.0 %all-to-all-start.1 = ((f32[64,32,256]{2,1,0:T(8,128)}), f32[64,32,256]{2,1,0:T(8,128)}, u32[]{:S(2)}, u32[]{:S(2)}) async-start(f32[64,32,256]{2,1,0:T(8,128)} %bitcast.31), calls=%async_computation.1 | async-start | bytes 4194304 | tf_op jit(solution)/shard_map/all_to_all | solution.py:29
  85.3 2.8 fusion.49
  88.1 2.0 fusion.48
  90.1 49.9 %all-gather.3.cloned.1.call-done = bf16[512,2048]{1,0:T(8,128)(2,1)} async-done(((bf16[512,256]{1,0:T(8,128)(2,1)}), bf16[512,2048]{1,0:T(8,128)(2,1)}) %all-gather.3.cloned.1.call-update) | async-done | bytes 2097168 | tf_op jit(solution)/shard_map/all_gather | solution.py:83
  140.0 3.6 %fusion.57 = f32[2048,256]{1,0:T(8,128)} fusion(bf16[512,2048]{1,0:T(8,128)(2,1)} %all-gather.3.cloned.1.call-done, bf16[512,256]{1,0:T(8,128)(2,1)S(1)} %get-tuple-element.90), kind=kOutput, calls=%fused_computation.74 | convolution fusion | flops 536870912 | bytes 4456448 | tf_op jit(solution)/shard_map/dot_general | solution.py:44
  143.7 10.2 %all-to-all-start = ((f32[64,32,256]{2,1,0:T(8,128)}), f32[64,32,256]{2,1,0:T(8,128)}, u32[]{:S(2)}, u32[]{:S(2)}) async-start(f32[64,32,256]{2,1,0:T(8,128)} %bitcast.30), calls=%async_computation | async-start | bytes 4194304 | tf_op jit(solution)/shard_map/all_to_all | solution.py:29
  153.9 0.3 dynamic_update_slice.29
  154.2 0.3 dynamic_update_slice.31
  156.5 0.3 dynamic_update_slice.27
  157.3 60.9 %all-reduce.10 = (f32[2048]{0:T(1024)S(1)}, f32[]{:T(128)}, f32[2048]{0:T(1024)S(1)}, f32[2048]{0:T(1024)S(1)}, f32[2048]{0:T(1024)S(1)}, /*index=5*/f32[2048]{0...) all-reduce(f32[2048]{0:T(1024)S(1)} %dynamic_update_slice.29, ...), channel_id=1, replica_groups=mesh['dp_0'=8,'dp_1'=4,'dp_2'=2,'feat_0'=4,'feat_1'=2] {'dp_0'}, use_global_device_ids=true, to_apply=%region_49.50 | all-reduce | flops 16386 | bytes 131088 | tf_op jit(solution)/shard_map/psum | solution.py:18
  218.2 14.7 %all-reduce.11 = (f32[2048]{0:T(1024)S(1)}, f32[]{:T(128)}, f32[2048]{0:T(1024)S(1)}, f32[2048]{0:T(1024)S(1)}, f32[2048]{0:T(1024)S(1)}, /*index=5*/f32[2048]{0...) all-reduce(f32[2048]{0:T(1024)S(1)} %get-tuple-element.17, ...), channel_id=1, replica_groups=mesh['dp_0'=8,'dp_1'=4,'dp_2'=2,'feat_0'=4,'feat_1'=2] {'dp_1'}, use_global_device_ids=true, to_apply=%region_50.51 | all-reduce | flops 16386 | bytes 131088 | tf_op jit(solution)/shard_map/psum | solution.py:18
  232.9 9.1 %all-reduce.12 = (f32[2048]{0:T(1024)S(1)}, f32[]{:T(128)}, f32[2048]{0:T(1024)S(1)}, f32[2048]{0:T(1024)S(1)}, f32[2048]{0:T(1024)S(1)}, /*index=5*/f32[2048]{0...) all-reduce(f32[2048]{0:T(1024)S(1)} %get-tuple-element.37, ...), channel_id=1, replica_groups=mesh['dp_0'=8,'dp_1'=4,'dp_2'=2,'feat_0'=4,'feat_1'=2] {'dp_2'}, use_global_device_ids=true, to_apply=%region_51.52 | all-reduce | flops 16386 | bytes 131088 | tf_op jit(solution)/shard_map/psum | solution.py:18
  242.0 18.6 %all-reduce.13 = (f32[2048]{0:T(1024)S(1)}, f32[]{:T(128)}, f32[2048]{0:T(1024)S(1)}, f32[2048]{0:T(1024)S(1)}, f32[2048]{0:T(1024)S(1)}, /*index=5*/f32[2048]{0...) all-reduce(f32[2048]{0:T(1024)S(1)} %get-tuple-element.57, ...), channel_id=1, replica_groups=mesh['dp_0'=8,'dp_1'=4,'dp_2'=2,'feat_0'=4,'feat_1'=2] {'feat_0'}, use_global_device_ids=true, to_apply=%region_52.53 | all-reduce | flops 16386 | bytes 131088 | tf_op jit(solution)/shard_map/psum | solution.py:18
  260.5 21.0 %all-reduce.14 = (f32[2048]{0:T(1024)S(1)}, f32[]{:T(128)}, f32[2048]{0:T(1024)S(1)}, f32[2048]{0:T(1024)S(1)}, f32[2048]{0:T(1024)S(1)}, /*index=5*/f32[2048]{0...) all-reduce(f32[2048]{0:T(1024)S(1)} %get-tuple-element.27, ...), channel_id=1, replica_groups=mesh['dp_0'=8,'dp_1'=4,'dp_2'=2,'feat_0'=4,'feat_1'=2] {'feat_1'}, use_global_device_ids=true, to_apply=%region_53.54 | all-reduce | flops 16386 | bytes 131088 | tf_op jit(solution)/shard_map/psum | solution.py:18
  281.5 0.7 add_sqrt_fusion.2
  282.2 0.7 add_sqrt_fusion.3
  282.9 0.7 add_sqrt_fusion
  283.6 0.7 add_sqrt_fusion.1
  284.3 1.7 reduce_sum.154
  286.0 0.7 fusion.53
  286.8 1.7 reduce_sum.146
  288.5 0.7 fusion.55
  289.1 0.6 pad_maximum_fusion
  (21 shorter events, 1.6 us)
Async XLA Ops:
  6.5 11.7 %copy-start = (bf16[5120,256]{1,0:T(8,128)(2,1)S(1)}, bf16[5120,256]{1,0:T(8,128)(2,1)}, u32[]{:S(2)}) copy-start(bf16[5120,256]{1,0:T(8,128)(2,1)} %param.4) | copy-start | bytes 7864324
  6.5 63.8 %all-gather.5.cloned.1.call-start = ((), (), s32[]{:S(2)}) async-start(), calls=%async_computation.3 | async-start | bytes 2359296 | tf_op jit(solution)/shard_map/all_gather | solution.py:83
  74.0 69.7 %all-to-all-start.1 = ((f32[64,32,256]{2,1,0:T(8,128)}), f32[64,32,256]{2,1,0:T(8,128)}, u32[]{:S(2)}, u32[]{:S(2)}) async-start(f32[64,32,256]{2,1,0:T(8,128)} %bitcast.31), calls=%async_computation.1 | async-start | bytes 4194304 | tf_op jit(solution)/shard_map/all_to_all | solution.py:29
  85.0 55.0 %all-gather.3.cloned.1.call-start = ((), (), s32[]{:S(2)}) async-start(), calls=%async_computation.2 | async-start | bytes 2359296 | tf_op jit(solution)/shard_map/all_gather | solution.py:83
  143.7 143.1 %all-to-all-start = ((f32[64,32,256]{2,1,0:T(8,128)}), f32[64,32,256]{2,1,0:T(8,128)}, u32[]{:S(2)}, u32[]{:S(2)}) async-start(f32[64,32,256]{2,1,0:T(8,128)} %bitcast.30), calls=%async_computation | async-start | bytes 4194304 | tf_op jit(solution)/shard_map/all_to_all | solution.py:29
Sparse Core Ops, SparseCore 0:
  21.2 49.1 all-gather.4
  88.2 51.8 all-gather.2
where the time goes:
time: 297 us
  blocking collectives  124 us (42%)
  waiting for transfers between devices  97.2 us (33%)
  starting transfers between devices  21.5 us (7%)
  other arithmetic  18.5 us (6%)
  matrix products  16.9 us (6%)
  between operations  14.7 us (5%)
  local copies, waits for them, and re-layouts  3.62 us (1%)
    psum x5, blocking collectives, one_axis_at_a_time(): array = lax.psum(array, axis)  124 us
    all_gather x2, waiting for transfers between devices, local(): lax.all_gather(second_rows, FEAT, axis=1, tiled=True)  97.2 us
    all_to_all x2, starting transfers between devices, summed_on_arrival(): lax.all_to_all(parts, axis, split_axis=0, concat_axis=0, tiled=True)  21.2 us
    dot_general x4, matrix products, select_rows(): jnp.dot(selection, embeddings, preferred_element_type=jnp.float32)  9.59 us
    dot_general x2, matrix products, image_product(): lax.dot_general(columns, first_rows, (((0,), (0,)), ((), ())), preferred_...  7.29 us
  transfers between devices with their start and end apart: 4, of which 2 were waited for; matrix products, arithmetic and copies ran while one was open for 6% of the time, Pallas kernels for 0%

commit v1 on v0

--- a/solution.py
+++ b/solution.py
@@ -15,7 +15,7 @@
 
 def one_axis_at_a_time(array, axes):
     for axis in axes:
-        array = lax.psum(array, axis)
+        array = jnp.sum(lax.all_gather(array, axis), axis=0)
     return array
 
 

time: 297 us -> 734 us (2.47)
  blocking collectives: 124 us -> 536 us
  local copies, waits for them, and re-layouts: 3.62 us -> 20.4 us
    all_gather x0 -> x40, blocking collectives: none -> 452 us  [one_axis_at_a_time(): array = jnp.sum(lax.all_gather(array, axis), axis=0)]
    psum x5 -> x0, blocking collectives: 124 us -> none  [one_axis_at_a_time(): array = lax.psum(array, axis)]
    unnamed x0 -> x5, blocking collectives: none -> 84.3 us
    unnamed x2 -> x35, local copies, waits for them, and re-layouts: 0.01 us -> 18.3 us
where the time goes in v1:
time: 734 us; the launch traced here: 733 us
  blocking collectives  536 us (73%)
  waiting for transfers between devices  97.2 us (13%)
  other arithmetic  25.8 us (4%)
  starting transfers between devices  21.5 us (3%)
  local copies, waits for them, and re-layouts  20.4 us (3%)
  matrix products  16.9 us (2%)
  between operations  15 us (2%)
    all_gather x40, blocking collectives, one_axis_at_a_time(): array = jnp.sum(lax.all_gather(array, axis), axis=0)  452 us
    all_gather x2, waiting for transfers between devices, local(): lax.all_gather(second_rows, FEAT, axis=1, tiled=True)  97.1 us
    unnamed x5, blocking collectives  84.3 us
    all_to_all x2, starting transfers between devices, summed_on_arrival(): lax.all_to_all(parts, axis, split_axis=0, concat_axis=0, tiled=True)  21.3 us
    unnamed x35, local copies, waits for them, and re-layouts  18.3 us
  transfers between devices with their start and end apart: 4, of which 2 were waited for; matrix products, arithmetic and copies ran while one was open for 6% of the time, Pallas kernels for 0%

profile of v1, /device:TPU:1, one launch (start us, length us, event | category | flops | bytes accessed | tf_op | source)
XLA Modules:
  0.0 732.7 jit_solution(6180170706636238449)
XLA Ops:
  23.1 47.3 %all-gather.43.cloned.1.call-done = bf16[512,2048]{1,0:T(8,128)(2,1)} async-done(((bf16[512,256]{1,0:T(8,128)(2,1)}), bf16[512,2048]{1,0:T(8,128)(2,1)}) %all-gather.43.cloned.1.call-update) | async-done | bytes 2097168 | tf_op jit(solution)/shard_map/all_gather | solution.py:83
  74.0 11.0 %all-to-all-start = ((f32[64,32,256]{2,1,0:T(8,128)}), f32[64,32,256]{2,1,0:T(8,128)}, u32[]{:S(2)}, u32[]{:S(2)}) async-start(f32[64,32,256]{2,1,0:T(8,128)} %bitcast.54), calls=%async_computation | async-start | bytes 4194304 | tf_op jit(solution)/shard_map/all_to_all | solution.py:29
  90.1 49.9 %all-gather.45.cloned.1.call-done = bf16[512,2048]{1,0:T(8,128)(2,1)} async-done(((bf16[512,256]{1,0:T(8,128)(2,1)}), bf16[512,2048]{1,0:T(8,128)(2,1)}) %all-gather.45.cloned.1.call-update) | async-done | bytes 2097168 | tf_op jit(solution)/shard_map/all_gather | solution.py:83
  143.6 10.3 %all-to-all-start.1 = ((f32[64,32,256]{2,1,0:T(8,128)}), f32[64,32,256]{2,1,0:T(8,128)}, u32[]{:S(2)}, u32[]{:S(2)}) async-start(f32[64,32,256]{2,1,0:T(8,128)} %bitcast.53), calls=%async_computation.1 | async-start | bytes 4194304 | tf_op jit(solution)/shard_map/all_to_all | solution.py:29
  157.8 49.9 %all-reduce.10 = (f32[8]{0:T(128)S(1)}, f32[8]{0:T(128)S(1)}) all-reduce(f32[8]{0:T(128)S(1)} %dynamic-update-slice.5, f32[8]{0:T(128)S(1)} %dynamic-update-slice), channel_id=1, replica_groups=mesh['dp_0'=8,'dp_1'=4,'dp_2'=2,'feat_0'=4,'feat_1'=2] {'dp_0'}, use_global_device_ids=true, to_apply=%add.5 | all-reduce | flops 16 | bytes 128
  234.7 11.0 %all-reduce.11 = (f32[4]{0:T(128)S(1)}, f32[4]{0:T(128)S(1)}) all-reduce(f32[4]{0:T(128)S(1)} %dynamic-update-slice.8, f32[4]{0:T(128)S(1)} %dynamic-update-slice.3), channel_id=1, replica_groups=mesh['dp_0'=8,'dp_1'=4,'dp_2'=2,'feat_0'=4,'feat_1'=2] {'feat_0'}, use_global_device_ids=true, to_apply=%add.8 | all-reduce | flops 8 | bytes 64
  250.8 11.8 %all-reduce.13 = (f32[2]{0:T(128)S(1)}, f32[2]{0:T(128)S(1)}) all-reduce(f32[2]{0:T(128)S(1)} %dynamic-update-slice.9, f32[2]{0:T(128)S(1)} %dynamic-update-slice.4), channel_id=1, replica_groups=mesh['dp_0'=8,'dp_1'=4,'dp_2'=2,'feat_0'=4,'feat_1'=2] {'feat_1'}, use_global_device_ids=true, to_apply=%add.9 | all-reduce | flops 4 | bytes 32
  262.7 18.5 %all-gather.33 = f32[8,1,2048]{2,1,0:T(1,128)S(1)} all-gather(f32[1,1,2048]{2,1,0:T(1,128)S(1)} %constant_dynamic-update-slice_fusion.6), channel_id=1, replica_groups=mesh['dp_0'=8,'dp_1'=4,'dp_2'=2,'feat_0'=4,'feat_1'=2] {'dp_0'}, dimensions={0}, use_global_device_ids=true | all-gather | bytes 73728 | tf_op jit(solution)/shard_map/all_gather | solution.py:18
  281.2 9.0 %all-gather.4 = f32[8192]{0:T(1024)S(1)} all-gather(f32[2048]{0:T(1024)S(1)} %reduce_sum.610), channel_id=6, replica_groups=mesh['dp_0'=8,'dp_1'=4,'dp_2'=2,'feat_0'=4,'feat_1'=2] {'dp_1'}, dimensions={0}, use_global_device_ids=true | all-gather | bytes 40960 | tf_op jit(solution)/shard_map/all_gather | solution.py:18
  293.8 11.0 %all-gather.6 = f32[8192]{0:T(1024)S(1)} all-gather(f32[2048]{0:T(1024)S(1)} %reduce_sum.612), channel_id=8, replica_groups=mesh['dp_0'=8,'dp_1'=4,'dp_2'=2,'feat_0'=4,'feat_1'=2] {'feat_0'}, dimensions={0}, use_global_device_ids=true | all-gather | bytes 40960 | tf_op jit(solution)/shard_map/all_gather | solution.py:18
  304.9 14.4 %all-gather.7 = f32[4096]{0:T(1024)S(1)} all-gather(f32[2048]{0:T(1024)S(1)} %reduce_sum.613), channel_id=9, replica_groups=mesh['dp_0'=8,'dp_1'=4,'dp_2'=2,'feat_0'=4,'feat_1'=2] {'feat_1'}, dimensions={0}, use_global_device_ids=true | all-gather | bytes 24576 | tf_op jit(solution)/shard_map/all_gather | solution.py:18
  319.3 18.5 %all-gather.35 = f32[8,1,2048]{2,1,0:T(1,128)S(1)} all-gather(f32[1,1,2048]{2,1,0:T(1,128)S(1)} %constant_dynamic-update-slice_fusion.4), channel_id=1, replica_groups=mesh['dp_0'=8,'dp_1'=4,'dp_2'=2,'feat_0'=4,'feat_1'=2] {'dp_0'}, dimensions={0}, use_global_device_ids=true | all-gather | bytes 73728 | tf_op jit(solution)/shard_map/all_gather | solution.py:18
  350.5 11.0 %all-gather.14 = f32[8192]{0:T(1024)S(1)} all-gather(f32[2048]{0:T(1024)S(1)} %reduce_sum.624), channel_id=16, replica_groups=mesh['dp_0'=8,'dp_1'=4,'dp_2'=2,'feat_0'=4,'feat_1'=2] {'feat_0'}, dimensions={0}, use_global_device_ids=true | all-gather | bytes 40960 | tf_op jit(solution)/shard_map/all_gather | solution.py:18
  361.5 14.4 %all-gather.15 = f32[4096]{0:T(1024)S(1)} all-gather(f32[2048]{0:T(1024)S(1)} %reduce_sum.625), channel_id=17, replica_groups=mesh['dp_0'=8,'dp_1'=4,'dp_2'=2,'feat_0'=4,'feat_1'=2] {'feat_1'}, dimensions={0}, use_global_device_ids=true | all-gather | bytes 24576 | tf_op jit(solution)/shard_map/all_gather | solution.py:18
  376.0 18.5 %all-gather.32 = f32[8,1,2048]{2,1,0:T(1,128)S(1)} all-gather(f32[1,1,2048]{2,1,0:T(1,128)S(1)} %constant_dynamic-update-slice_fusion.7), channel_id=1, replica_groups=mesh['dp_0'=8,'dp_1'=4,'dp_2'=2,'feat_0'=4,'feat_1'=2] {'dp_0'}, dimensions={0}, use_global_device_ids=true | all-gather | bytes 73728 | tf_op jit(solution)/shard_map/all_gather | solution.py:18
  407.2 11.0 %all-gather.2 = f32[8192]{0:T(1024)S(1)} all-gather(f32[2048]{0:T(1024)S(1)} %reduce_sum.606), channel_id=4, replica_groups=mesh['dp_0'=8,'dp_1'=4,'dp_2'=2,'feat_0'=4,'feat_1'=2] {'feat_0'}, dimensions={0}, use_global_device_ids=true | all-gather | bytes 40960 | tf_op jit(solution)/shard_map/all_gather | solution.py:18
  418.2 14.4 %all-gather.3 = f32[4096]{0:T(1024)S(1)} all-gather(f32[2048]{0:T(1024)S(1)} %reduce_sum.607), channel_id=5, replica_groups=mesh['dp_0'=8,'dp_1'=4,'dp_2'=2,'feat_0'=4,'feat_1'=2] {'feat_1'}, dimensions={0}, use_global_device_ids=true | all-gather | bytes 24576 | tf_op jit(solution)/shard_map/all_gather | solution.py:18
  432.7 18.5 %all-gather.34 = f32[8,1,2048]{2,1,0:T(1,128)S(1)} all-gather(f32[1,1,2048]{2,1,0:T(1,128)S(1)} %constant_dynamic-update-slice_fusion.5), channel_id=1, replica_groups=mesh['dp_0'=8,'dp_1'=4,'dp_2'=2,'feat_0'=4,'feat_1'=2] {'dp_0'}, dimensions={0}, use_global_device_ids=true | all-gather | bytes 73728 | tf_op jit(solution)/shard_map/all_gather | solution.py:18
  463.8 11.0 %all-gather.10 = f32[8192]{0:T(1024)S(1)} all-gather(f32[2048]{0:T(1024)S(1)} %reduce_sum.618), channel_id=12, replica_groups=mesh['dp_0'=8,'dp_1'=4,'dp_2'=2,'feat_0'=4,'feat_1'=2] {'feat_0'}, dimensions={0}, use_global_device_ids=true | all-gather | bytes 40960 | tf_op jit(solution)/shard_map/all_gather | solution.py:18
  474.9 14.4 %all-gather.11 = f32[4096]{0:T(1024)S(1)} all-gather(f32[2048]{0:T(1024)S(1)} %reduce_sum.619), channel_id=13, replica_groups=mesh['dp_0'=8,'dp_1'=4,'dp_2'=2,'feat_0'=4,'feat_1'=2] {'feat_1'}, dimensions={0}, use_global_device_ids=true | all-gather | bytes 24576 | tf_op jit(solution)/shard_map/all_gather | solution.py:18
  489.3 18.5 %all-gather.36 = f32[8,1,2048]{2,1,0:T(1,128)S(1)} all-gather(f32[1,1,2048]{2,1,0:T(1,128)S(1)} %constant_dynamic-update-slice_fusion.3), channel_id=1, replica_groups=mesh['dp_0'=8,'dp_1'=4,'dp_2'=2,'feat_0'=4,'feat_1'=2] {'dp_0'}, dimensions={0}, use_global_device_ids=true | all-gather | bytes 73728 | tf_op jit(solution)/shard_map/all_gather | solution.py:18
  520.5 11.1 %all-gather.18 = f32[8192]{0:T(1024)S(1)} all-gather(f32[2048]{0:T(1024)S(1)} %reduce_sum.639), channel_id=20, replica_groups=mesh['dp_0'=8,'dp_1'=4,'dp_2'=2,'feat_0'=4,'feat_1'=2] {'feat_0'}, dimensions={0}, use_global_device_ids=true | all-gather | bytes 40960 | tf_op jit(solution)/shard_map/all_gather | solution.py:18
  531.6 14.6 %all-gather.19 = f32[4096]{0:T(1024)S(1)} all-gather(f32[2048]{0:T(1024)S(1)} %reduce_sum.640), channel_id=21, replica_groups=mesh['dp_0'=8,'dp_1'=4,'dp_2'=2,'feat_0'=4,'feat_1'=2] {'feat_1'}, dimensions={0}, use_global_device_ids=true | all-gather | bytes 24576 | tf_op jit(solution)/shard_map/all_gather | solution.py:18
  546.2 18.5 %all-gather.38 = f32[8,1,2048]{2,1,0:T(1,128)S(1)} all-gather(f32[1,1,2048]{2,1,0:T(1,128)S(1)} %constant_dynamic-update-slice_fusion.1), channel_id=1, replica_groups=mesh['dp_0'=8,'dp_1'=4,'dp_2'=2,'feat_0'=4,'feat_1'=2] {'dp_0'}, dimensions={0}, use_global_device_ids=true | all-gather | bytes 73728 | tf_op jit(solution)/shard_map/all_gather | solution.py:18
  577.4 11.0 %all-gather.26 = f32[8192]{0:T(1024)S(1)} all-gather(f32[2048]{0:T(1024)S(1)} %reduce_sum.651), channel_id=28, replica_groups=mesh['dp_0'=8,'dp_1'=4,'dp_2'=2,'feat_0'=4,'feat_1'=2] {'feat_0'}, dimensions={0}, use_global_device_ids=true | all-gather | bytes 40960 | tf_op jit(solution)/shard_map/all_gather | solution.py:18
  588.4 14.4 %all-gather.27 = f32[4096]{0:T(1024)S(1)} all-gather(f32[2048]{0:T(1024)S(1)} %reduce_sum.652), channel_id=29, replica_groups=mesh['dp_0'=8,'dp_1'=4,'dp_2'=2,'feat_0'=4,'feat_1'=2] {'feat_1'}, dimensions={0}, use_global_device_ids=true | all-gather | bytes 24576 | tf_op jit(solution)/shard_map/all_gather | solution.py:18
  602.9 18.5 %all-gather.37 = f32[8,1,2048]{2,1,0:T(1,128)S(1)} all-gather(f32[1,1,2048]{2,1,0:T(1,128)S(1)} %constant_dynamic-update-slice_fusion.2), channel_id=1, replica_groups=mesh['dp_0'=8,'dp_1'=4,'dp_2'=2,'feat_0'=4,'feat_1'=2] {'dp_0'}, dimensions={0}, use_global_device_ids=true | all-gather | bytes 73728 | tf_op jit(solution)/shard_map/all_gather | solution.py:18
  634.0 11.0 %all-gather.22 = f32[8192]{0:T(1024)S(1)} all-gather(f32[2048]{0:T(1024)S(1)} %reduce_sum.645), channel_id=24, replica_groups=mesh['dp_0'=8,'dp_1'=4,'dp_2'=2,'feat_0'=4,'feat_1'=2] {'feat_0'}, dimensions={0}, use_global_device_ids=true | all-gather | bytes 40960 | tf_op jit(solution)/shard_map/all_gather | solution.py:18
  645.1 14.4 %all-gather.23 = f32[4096]{0:T(1024)S(1)} all-gather(f32[2048]{0:T(1024)S(1)} %reduce_sum.646), channel_id=25, replica_groups=mesh['dp_0'=8,'dp_1'=4,'dp_2'=2,'feat_0'=4,'feat_1'=2] {'feat_1'}, dimensions={0}, use_global_device_ids=true | all-gather | bytes 24576 | tf_op jit(solution)/shard_map/all_gather | solution.py:18
  659.5 18.5 %all-gather.39 = f32[8,1,2048]{2,1,0:T(1,128)S(1)} all-gather(f32[1,1,2048]{2,1,0:T(1,128)S(1)} %constant_dynamic-update-slice_fusion), channel_id=1, replica_groups=mesh['dp_0'=8,'dp_1'=4,'dp_2'=2,'feat_0'=4,'feat_1'=2] {'dp_0'}, dimensions={0}, use_global_device_ids=true | all-gather | bytes 73728 | tf_op jit(solution)/shard_map/all_gather | solution.py:18
  690.7 10.9 %all-gather.30 = f32[8192]{0:T(1024)S(1)} all-gather(f32[2048]{0:T(1024)S(1)} %reduce_sum.657), channel_id=32, replica_groups=mesh['dp_0'=8,'dp_1'=4,'dp_2'=2,'feat_0'=4,'feat_1'=2] {'feat_0'}, dimensions={0}, use_global_device_ids=true | all-gather | bytes 40960 | tf_op jit(solution)/shard_map/all_gather | solution.py:18
  701.7 14.5 %all-gather.31 = f32[4096]{0:T(1024)S(1)} all-gather(f32[2048]{0:T(1024)S(1)} %reduce_sum.658), channel_id=33, replica_groups=mesh['dp_0'=8,'dp_1'=4,'dp_2'=2,'feat_0'=4,'feat_1'=2] {'feat_1'}, dimensions={0}, use_global_device_ids=true | all-gather | bytes 24576 | tf_op jit(solution)/shard_map/all_gather | solution.py:18
  (168 shorter events, 165.9 us)
Async XLA Ops:
  6.5 11.7 %copy-start = (bf16[5120,256]{1,0:T(8,128)(2,1)S(1)}, bf16[5120,256]{1,0:T(8,128)(2,1)}, u32[]{:S(2)}) copy-start(bf16[5120,256]{1,0:T(8,128)(2,1)} %param.4) | copy-start | bytes 7864324
  6.5 63.8 %all-gather.43.cloned.1.call-start = ((), (), s32[]{:S(2)}) async-start(), calls=%async_computation.2 | async-start | bytes 2359296 | tf_op jit(solution)/shard_map/all_gather | solution.py:83
  74.0 69.6 %all-to-all-start = ((f32[64,32,256]{2,1,0:T(8,128)}), f32[64,32,256]{2,1,0:T(8,128)}, u32[]{:S(2)}, u32[]{:S(2)}) async-start(f32[64,32,256]{2,1,0:T(8,128)} %bitcast.54), calls=%async_computation | async-start | bytes 4194304 | tf_op jit(solution)/shard_map/all_to_all | solution.py:29
  85.0 54.9 %all-gather.45.cloned.1.call-start = ((), (), s32[]{:S(2)}) async-start(), calls=%async_computation.3 | async-start | bytes 2359296 | tf_op jit(solution)/shard_map/all_gather | solution.py:83
  143.6 579.2 %all-to-all-start.1 = ((f32[64,32,256]{2,1,0:T(8,128)}), f32[64,32,256]{2,1,0:T(8,128)}, u32[]{:S(2)}, u32[]{:S(2)}) async-start(f32[64,32,256]{2,1,0:T(8,128)} %bitcast.53), calls=%async_computation.1 | async-start | bytes 4194304 | tf_op jit(solution)/shard_map/all_to_all | solution.py:29
Sparse Core Ops, SparseCore 0:
  21.2 49.1 all-gather.42
  88.2 51.7 all-gather.44
